TPU v7x, 32 devices: a whole 2x2x4 slice. The times are simulated.
32 devices in a mesh: seq: 16 (over z, y, core), fsdp: 2 (over x).
Axes of the slice: x: 2, y: 2, z: 4, core: 2. Of those that a mesh axis runs over, the one named last changes fastest.
Arguments:
- tokens: bfloat16 [64, 8192], P('seq', 'fsdp'), may hold values from -6 to 6
- gate_weight: bfloat16 [8192, 16384], P('fsdp', 'seq'), may hold values from -0.0625 to 0.0625
- up_weight: bfloat16 [8192, 16384], P('fsdp', 'seq'), may hold values from -0.0625 to 0.0625
- down_weight: bfloat16 [8192, 16384], P('fsdp', 'seq'), may hold values from -0.046875 to 0.046875
Outputs:
- mixed_out: bfloat16 [64, 8192], P('seq', 'fsdp')
All inputs are finite; a program needn't handle non-finite values.
Results may differ from a plain program's by a relative error of at most 0.0049.
Values may be sent and summed in bfloat16 or wider, within the bound.
A program may use at most 64 MiB of HBM per device.

v0:
```python
import jax
import jax.numpy as jnp
from jax import lax
from jax.sharding import PartitionSpec as P


def project_down(hidden, weight):
    return lax.dot_general(
        hidden, weight, (((1,), (1,)), ((), ())), preferred_element_type=jnp.float32
    )


def on_device(tokens, gate_weight, up_weight, down_weight):
    units = gate_weight.shape[1]
    paired = jnp.concatenate([gate_weight, up_weight], axis=1)
    parts = jnp.dot(
        lax.all_gather(tokens, "seq", axis=0, tiled=True),
        paired,
        preferred_element_type=jnp.float32,
    )
    values = lax.psum(parts, "fsdp")
    hidden = (jax.nn.silu(values[:, :units]) * values[:, units:]).astype(jnp.bfloat16)
    return lax.psum_scatter(
        project_down(hidden, down_weight), "seq", scatter_dimension=0, tiled=True
    ).astype(jnp.bfloat16)


def solution(mesh):
    return jax.shard_map(
        on_device,
        mesh=mesh,
        in_specs=(P("seq", "fsdp"), P("fsdp", "seq"), P("fsdp", "seq"), P("fsdp", "seq")),
        out_specs=P("seq", "fsdp"),
        check_vma=False,
    )
```

profile of v0, /device:TPU:0, one launch (start us, length us, event | category | flops | bytes accessed | tf_op | source)
XLA Modules:
  0.0 152.2 jit_solution(14321686645150590111)
XLA Ops:
  6.5 0.0 all-reduce.4.cloned.1.call-start
  6.5 24.8 %all-gather = bf16[16,4,4096]{2,1,0:T(4,128)(2,1)S(1)} all-gather(bf16[1,4,4096]{2,1,0:T(4,128)(2,1)} %bitcast.6), channel_id=1, replica_groups=mesh['seq'=16,'fsdp'=2] {'seq'}, dimensions={0}, use_global_device_ids=true | all-gather | bytes 557056 | tf_op jit(solution)/shard_map/all_gather | solution.py:17
  31.3 0.1 reshape.1
  31.5 0.0 copy-start
  31.5 8.2 %fusion.4 = f32[64,2048]{1,0:T(8,128)} fusion(bf16[64,4096]{1,0:T(8,128)(2,1)S(1)} %reshape.1, bf16[4096,1024]{1,0:T(8,128)(2,1)} %param.6, bf16[4096,1024]{1,0:T(8,128)(2,1)} %param.5), kind=kOutput, calls=%fused_computation.4 | convolution fusion | flops 1107296256 | bytes 17825792 | tf_op jit(solution)/shard_map/dot_general | solution.py:16
  39.7 0.0 all-reduce.4.cloned.1.call-update
  39.8 0.0 copy-done
  39.8 0.6 dynamic-slice
  41.0 24.8 %all-reduce.4.cloned.1.call-done = f32[64,2048]{1,0:T(8,128)} async-done(((f32[64,2048]{1,0:T(8,128)}), f32[64,2048]{1,0:T(8,128)}) %all-reduce.4.cloned.1.call-update) | async-done | bytes 524304 | tf_op jit(solution)/shard_map/psum | solution.py:21
  65.8 6.2 %fusion.8 = f32[64,4096]{1,0:T(8,128)S(1)} fusion(bf16[4096,1024]{1,0:T(8,128)(2,1)} %param.7, f32[64,2048]{1,0:T(8,128)} %all-reduce.4.cloned.1.call-done), kind=kOutput, calls=%fused_computation.7 | convolution fusion | flops 537264128 | bytes 9961472 | tf_op jit(solution)/shard_map/dot_general | solution.py:8
  72.0 72.7 %all-reduce.5 = bf16[64,4096]{1,0:T(8,128)(2,1)S(1)} all-reduce(f32[64,4096]{1,0:T(8,128)S(1)} %fusion.8), channel_id=2, replica_groups=mesh['seq'=16,'fsdp'=2] {'seq'}, use_global_device_ids=true, to_apply=%region_1.2.clone | all-reduce | flops 262144 | bytes 1572864
  144.7 0.6 dynamic-slice_convert_fusion
Async XLA Ops:
  6.5 59.3 %all-reduce.4.cloned.1.call-start = ((), (), s32[]{:S(2)}) async-start(), calls=%async_computation | async-start | bytes 1048576 | tf_op jit(solution)/shard_map/psum | solution.py:21
  31.5 8.3 %copy-start = (u32[32]{0:T(128)S(1)}, u32[32]{0:T(128)}, u32[]{:S(2)}) copy-start(u32[32]{0:T(128)} %constant.6) | copy-start | bytes 388
Sparse Core Ops, SparseCore 0:
  39.9 25.8 all-reduce.3
where the time goes:
time: 152 us
  blocking collectives  97.5 us (64%)
  waiting for transfers between devices  24.8 us (16%)
  matrix products  14.5 us (10%)
  between operations  14.1 us (9%)
    unnamed x1, blocking collectives  72.7 us
    all_gather x1, blocking collectives, on_device(): lax.all_gather(tokens, 'seq', axis=0, tiled=True)  24.8 us
    psum x1, waiting for transfers between devices, on_device(): values = lax.psum(parts, 'fsdp')  24.8 us
    dot_general x1, matrix products, on_device(): jnp.dot(lax.all_gather(tokens, 'seq', axis=0, tiled=True), paired, prefer...  8.25 us
    dot_general x1, matrix products, project_down(): lax.dot_general(hidden, weight, (((1,), (1,)), ((), ())), preferred_eleme...  6.22 us
  transfers between devices with their start and end apart: 1, of which 1 were waited for; matrix products, arithmetic and copies ran while one was open for 0% of the time, Pallas kernels for 0%

commit v1 on v0

v1 whole, which is shorter than its diff:
```python
import functools

import jax
import jax.numpy as jnp
from jax import lax
from jax.experimental import pallas as pl
from jax.experimental.pallas import tpu as pltpu
from jax.sharding import PartitionSpec as P

MESH = pl.DeviceIdType.MESH
F32, BF16 = jnp.float32, jnp.bfloat16
KC, FC = 2, 4


def ffn(R, T, UC, tok, wg, wu, wd, out, G, X, VG, VU, VD, A, SX, RX, H, O, RC, SY, RY,
        S2, SZ, RZ, wsem, dsem, tsem, gz, gy, gc, gr, xs, xr, cs, cr, ys, yr, zs, zr):
    idx, x = lax.axis_index("seq"), lax.axis_index("fsdp")
    c, y, r = lax.rem(idx, 2), lax.rem(lax.div(idx, 2), 2), lax.div(idx, 4)
    core_peer = (idx + 1 - 2 * c, x)
    y_peer = (idx + 2 - 4 * y, x)
    x_peer = (idx, 1 - x)
    away = [lax.rem(r + d, R) for d in range(R)]
    z_peer = [(rr * 4 + y * 2 + c, x) for rr in away]
    kw, fw, uw = G.shape[-1], O.shape[-1], SX.shape[-1]
    rows = X.shape[1]
    mine = R * T

    toks = [pltpu.make_async_copy(tok.at[:, pl.ds(k * kw, kw)], G.at[k, c, y, r], tsem.at[k]) for k in range(KC)]
    for t in toks:
        t.start()
    weights = []
    for k in range(KC):
        part = pl.ds(k * kw, kw)
        weights.append([pltpu.make_async_copy(w.at[part], v.at[part], wsem.at[i, k]) for i, (w, v) in enumerate(((wg, VG), (wu, VU)))])
        for w in weights[-1]:
            w.start()
    downs = []
    for f in range(FC):
        part = pl.ds(f * fw, fw)
        downs.append(pltpu.make_async_copy(wd.at[part], VD.at[part], dsem.at[f]))
        downs[-1].start()

    barrier = pltpu.get_barrier_semaphore()
    peers = z_peer[1:] + [y_peer, core_peer, x_peer]
    for p in peers:
        pl.semaphore_signal(barrier, inc=1, device_id=p, device_id_type=MESH)
    pl.semaphore_wait(barrier, len(peers))

    sent = []

    def send(src, dst, s, q, peer):
        copy = pltpu.make_async_remote_copy(src_ref=src, dst_ref=dst, send_sem=s, recv_sem=q, device_id=peer, device_id_type=MESH)
        copy.start()
        sent.append(copy)

    def await_block(k, cc, yy, rr):
        g = G.at[k, cc, yy, rr]
        pltpu.make_async_remote_copy(src_ref=g, dst_ref=g, send_sem=gz.at[k, 0], recv_sem=gr.at[k, cc, yy, rr],
                                     device_id=core_peer, device_id_type=MESH).wait_recv()

    def to_peer(k, yy, rr, s, peer):
        g = G.at[k, c, yy, rr]
        send(g, g, s, gr.at[k, c, yy, rr], peer)

    for k in range(KC):
        toks[k].wait()
        for d in range(1, R):
            to_peer(k, y, r, gz.at[k, d], z_peer[d])
        to_peer(k, y, r, gy.at[k, 0], y_peer)
        to_peer(k, y, r, gc.at[k, 0, 0], core_peer)
    for k in range(KC):
        for d in range(1, R):
            await_block(k, c, y, away[d])
            to_peer(k, y, away[d], gy.at[k, d], y_peer)
            to_peer(k, y, away[d], gc.at[k, 0, d], core_peer)
    for k in range(KC):
        for d in range(R):
            await_block(k, c, 1 - y, away[d])
            to_peer(k, 1 - y, away[d], gc.at[k, 1, d], core_peer)
    for k in range(KC):
        for yy in (y, 1 - y):
            for d in range(R):
                await_block(k, 1 - c, yy, away[d])
        for cc in range(2):
            for yy in range(2):
                at = (cc * 2 + yy) * mine
                X[k, at:at + mine, :] = G[k, cc, yy].reshape(mine, kw)
        for w in weights[k]:
            w.wait()
        for u in range(UC):
            cols = pl.ds(u * uw, uw)
            for i, v in enumerate((VG, VU)):
                value = jnp.dot(X[k], v[pl.ds(k * kw, kw), cols], preferred_element_type=F32)
                if k > 0:
                    value += A[i, :, cols]
                A[i, :, cols] = value
                if k == KC - 1:
                    SX[u, i] = value.astype(BF16)
            if k == KC - 1:
                send(SX.at[u], RX.at[u], xs.at[u], xr.at[u], x_peer)

    def await_x(u):
        pltpu.make_async_remote_copy(src_ref=SX.at[u], dst_ref=RX.at[u], send_sem=xs.at[u], recv_sem=xr.at[u],
                                     device_id=x_peer, device_id_type=MESH).wait_recv()

    def down(f, lo, hi):
        return lax.dot_general(H[:, lo:hi], VD[pl.ds(f * fw, fw), lo:hi], (((1,), (1,)), ((), ())),
                               preferred_element_type=F32).reshape(2, 2, mine, fw)

    def hidden(u):
        await_x(u)
        cols = pl.ds(u * uw, uw)
        gate = A[0, :, cols] + RX[u, 0].astype(F32)
        up = A[1, :, cols] + RX[u, 1].astype(F32)
        H[:, cols] = (gate / (1.0 + jnp.exp(-gate)) * up).astype(BF16)

    half = UC // 2
    for u in range(half):
        hidden(u)
    for f in range(FC):
        downs[f].wait()
        if half:
            O[f] = down(f, 0, half * uw)
    for u in range(half, UC):
        hidden(u)

    arrivals = {}

    def to_core(f):
        value = down(f, half * uw, UC * uw)
        O[f] = O[f] + value if half else value
        send(O.at[f, 1 - c], RC.at[f], cs.at[f], cr.at[f], core_peer)
        arrivals["c", f] = sent[-1]

    def to_y(f):
        arrivals["c", f].wait_recv()
        SY[f] = (O[f, c, 1 - y] + RC[f, 1 - y]).astype(BF16)
        send(SY.at[f], RY.at[f], ys.at[f], yr.at[f], y_peer)
        arrivals["y", f] = sent[-1]

    def to_z(f):
        arrivals["y", f].wait_recv()
        total = (O[f, c, y] + RC[f, y] + RY[f].astype(F32)).reshape(R, T, fw)
        S2[f] = total
        SZ[f] = total.astype(BF16)
        for d in range(1, R):
            send(SZ.at[f, away[d]], RZ.at[f, d], zs.at[f, d], zr.at[f, d], z_peer[d])
            arrivals["z", f, d] = sent[-1]

    def finish(f):
        total = S2[f, r]
        for d in range(1, R):
            arrivals["z", f, d].wait_recv()
            total += RZ[f, d].astype(F32)
        out[:, pl.ds(f * fw, fw)] = total.astype(BF16)

    for f in range(FC):
        to_core(f)
        if f:
            to_y(f - 1)
    to_y(FC - 1)
    for f in range(FC):
        to_z(f)
    for f in range(FC):
        finish(f)
    for copy in sent:
        copy.wait_send()


def solution(mesh):
    n = mesh.shape["seq"]

    def on_device(tok, wg, wu, wd):
        T, K = tok.shape
        U = wg.shape[1]
        F = wd.shape[0]
        R = n // 4
        UC = max(1, U // 256)
        uw, kw, fw, rows, mine = U // UC, K // KC, F // FC, n * T, R * T
        dma = pltpu.SemaphoreType.DMA
        scratch = [
            pltpu.VMEM((KC, 2, 2, R, T, kw), BF16),
            pltpu.VMEM((KC, rows, kw), BF16),
            pltpu.VMEM((K, U), BF16),
            pltpu.VMEM((K, U), BF16),
            pltpu.VMEM((F, U), BF16),
            pltpu.VMEM((2, rows, U), F32),
            pltpu.VMEM((UC, 2, rows, uw), BF16),
            pltpu.VMEM((UC, 2, rows, uw), BF16),
            pltpu.VMEM((rows, U), BF16),
            pltpu.VMEM((FC, 2, 2, mine, fw), F32),
            pltpu.VMEM((FC, 2, mine, fw), F32),
            pltpu.VMEM((FC, mine, fw), BF16),
            pltpu.VMEM((FC, mine, fw), BF16),
            pltpu.VMEM((FC, R, T, fw), F32),
            pltpu.VMEM((FC, R, T, fw), BF16),
            pltpu.VMEM((FC, R, T, fw), BF16),
            dma((2, KC)), dma((FC,)), dma((KC,)),
            dma((KC, R)), dma((KC, R)), dma((KC, 2, R)), dma((KC, 2, 2, R)),
            dma((UC,)), dma((UC,)),
            dma((FC,)), dma((FC,)), dma((FC,)), dma((FC,)), dma((FC, R)), dma((FC, R)),
        ]
        return pl.pallas_call(
            functools.partial(ffn, R, T, UC),
            out_shape=jax.ShapeDtypeStruct((T, F), BF16),
            in_specs=[pl.BlockSpec(memory_space=pl.ANY)] * 4,
            out_specs=pl.BlockSpec(memory_space=pltpu.VMEM),
            scratch_shapes=scratch,
            compiler_params=pltpu.CompilerParams(
                collective_id=0, has_side_effects=True, vmem_limit_bytes=60 * 1024 * 1024
            ),
        )(tok, wg, wu, wd)

    return jax.shard_map(
        on_device,
        mesh=mesh,
        in_specs=(P("seq", "fsdp"), P("fsdp", "seq"), P("fsdp", "seq"), P("fsdp", "seq")),
        out_specs=P("seq", "fsdp"),
        check_vma=False,
    )
```

time: 152 us -> 40.4 us (0.27)
  blocking collectives: 97.5 us -> 0 us
  Pallas kernels: 0 us -> 38.8 us
  waiting for transfers between devices: 24.8 us -> 0 us
  matrix products: 14.5 us -> 0 us
  between operations: 14.1 us -> 0.01 us
    unnamed x1 -> x0, blocking collectives: 72.7 us -> none
    pallas_call x0 -> x1, Pallas kernels: none -> 38.8 us  [on_device(): pl.pallas_call(functools.partial(ffn, R, T, UC), out_shape=jax.ShapeDtype...]
    all_gather x1 -> x0, blocking collectives: 24.8 us -> none  [on_device(): lax.all_gather(tokens, 'seq', axis=0, tiled=True)]
    psum x1 -> x0, waiting for transfers between devices: 24.8 us -> none  [on_device(): values = lax.psum(parts, 'fsdp')]
    dot_general x2 -> x0, matrix products: 14.5 us -> none  [the longest x1 8.25 us: on_device(): jnp.dot(lax.all_gather(tokens, 'seq', axis=0, tiled=True), paired, prefer...]
  transfers between devices with their start and end apart: 1 -> 0, of which waited for: 1 -> 0; matrix products, arithmetic and copies ran while one was open for 0% -> 0% of each run, Pallas kernels for 0% -> 0%
where the time goes in v1:
time: 40.4 us; the launch traced here: 40.2 us
  Pallas kernels  38.8 us (96%)
  local copies, waits for them, and re-layouts  1.39 us (3%)
    pallas_call x1, Pallas kernels, on_device(): pl.pallas_call(functools.partial(ffn, R, T, UC), out_shape=jax.ShapeDtype...  38.8 us
    unnamed x1, local copies, waits for them, and re-layouts  1.39 us

profile of v1, /device:TPU:0, one launch (start us, length us, event | category | flops | bytes accessed | tf_op | source)
XLA Modules:
  0.0 40.2 jit_solution(17532257582705783315)
XLA Ops:
  0.0 38.8 %shard_map.46 = bf16[4,4096]{1,0:T(4,128)(2,1)} custom-call(bf16[4,4096]{1,0:T(4,128)(2,1)} %tok.1, bf16[4096,1024]{1,0:T(8,128)(2,1)} %wg.1, bf16[4096,1024]{1,0:T(8,128)(2,1)} %wu.1, bf16[4096,1024]{1,0:T(8,128)(2,1)} %wd.1), custom_call_target="tpu_custom_call" | custom-call | tf_op jit(solution)/shard_map/pallas_call | solution.py:203
  38.8 1.4 %copy.6 = bf16[4,4096]{1,0:T(4,128)(2,1)} copy(bf16[4,4096]{1,0:T(4,128)(2,1)} %shard_map.46) | data formatting | bytes 65536

commit v2 on v1

--- a/solution.py
+++ b/solution.py
@@ -9,7 +9,7 @@
 
 MESH = pl.DeviceIdType.MESH
 F32, BF16 = jnp.float32, jnp.bfloat16
-KC, FC = 2, 4
+KC, FC = 4, 4
 
 
 def ffn(R, T, UC, tok, wg, wu, wd, out, G, X, VG, VU, VD, A, SX, RX, H, O, RC, SY, RY,
@@ -28,6 +28,34 @@
     toks = [pltpu.make_async_copy(tok.at[:, pl.ds(k * kw, kw)], G.at[k, c, y, r], tsem.at[k]) for k in range(KC)]
     for t in toks:
         t.start()
+    barrier = pltpu.get_barrier_semaphore()
+    peers = z_peer[1:] + [y_peer, core_peer, x_peer]
+    for p in peers:
+        pl.semaphore_signal(barrier, inc=1, device_id=p, device_id_type=MESH)
+    pl.semaphore_wait(barrier, len(peers))
+
+    sent = []
+
+    def send(src, dst, s, q, peer):
+        copy = pltpu.make_async_remote_copy(src_ref=src, dst_ref=dst, send_sem=s, recv_sem=q, device_id=peer, device_id_type=MESH)
+        copy.start()
+        sent.append(copy)
+
+    def await_block(k, cc, yy, rr):
+        g = G.at[k, cc, yy, rr]
+        pltpu.make_async_remote_copy(src_ref=g, dst_ref=g, send_sem=gz.at[k, 0], recv_sem=gr.at[k, cc, yy, rr],
+                                     device_id=core_peer, device_id_type=MESH).wait_recv()
+
+    def to_peer(k, yy, rr, s, peer):
+        g = G.at[k, c, yy, rr]
+        send(g, g, s, gr.at[k, c, yy, rr], peer)
+
+    for k in range(KC):
+        toks[k].wait()
+        for d in range(1, R):
+            to_peer(k, y, r, gz.at[k, d], z_peer[d])
+        to_peer(k, y, r, gy.at[k, 0], y_peer)
+        to_peer(k, y, r, gc.at[k, 0, 0], core_peer)
     weights = []
     for k in range(KC):
         part = pl.ds(k * kw, kw)
@@ -40,34 +68,6 @@
         downs.append(pltpu.make_async_copy(wd.at[part], VD.at[part], dsem.at[f]))
         downs[-1].start()
 
-    barrier = pltpu.get_barrier_semaphore()
-    peers = z_peer[1:] + [y_peer, core_peer, x_peer]
-    for p in peers:
-        pl.semaphore_signal(barrier, inc=1, device_id=p, device_id_type=MESH)
-    pl.semaphore_wait(barrier, len(peers))
-
-    sent = []
-
-    def send(src, dst, s, q, peer):
-        copy = pltpu.make_async_remote_copy(src_ref=src, dst_ref=dst, send_sem=s, recv_sem=q, device_id=peer, device_id_type=MESH)
-        copy.start()
-        sent.append(copy)
-
-    def await_block(k, cc, yy, rr):
-        g = G.at[k, cc, yy, rr]
-        pltpu.make_async_remote_copy(src_ref=g, dst_ref=g, send_sem=gz.at[k, 0], recv_sem=gr.at[k, cc, yy, rr],
-                                     device_id=core_peer, device_id_type=MESH).wait_recv()
-
-    def to_peer(k, yy, rr, s, peer):
-        g = G.at[k, c, yy, rr]
-        send(g, g, s, gr.at[k, c, yy, rr], peer)
-
-    for k in range(KC):
-        toks[k].wait()
-        for d in range(1, R):
-            to_peer(k, y, r, gz.at[k, d], z_peer[d])
-        to_peer(k, y, r, gy.at[k, 0], y_peer)
-        to_peer(k, y, r, gc.at[k, 0, 0], core_peer)
     for k in range(KC):
         for d in range(1, R):
             await_block(k, c, y, away[d])
@@ -114,21 +114,23 @@
         up = A[1, :, cols] + RX[u, 1].astype(F32)
         H[:, cols] = (gate / (1.0 + jnp.exp(-gate)) * up).astype(BF16)
 
-    half = UC // 2
-    for u in range(half):
+    for u in range(UC - 1):
         hidden(u)
-    for f in range(FC):
-        downs[f].wait()
-        if half:
-            O[f] = down(f, 0, half * uw)
-    for u in range(half, UC):
-        hidden(u)
+        for f in range(FC):
+            if u == 0:
+                downs[f].wait()
+            value = down(f, u * uw, (u + 1) * uw)
+            O[f] = O[f] + value if u else value
+    hidden(UC - 1)
+    if UC == 1:
+        for f in range(FC):
+            downs[f].wait()
 
     arrivals = {}
 
     def to_core(f):
-        value = down(f, half * uw, UC * uw)
-        O[f] = O[f] + value if half else value
+        value = down(f, (UC - 1) * uw, UC * uw)
+        O[f] = O[f] + value if UC > 1 else value
         send(O.at[f, 1 - c], RC.at[f], cs.at[f], cr.at[f], core_peer)
         arrivals["c", f] = sent[-1]
 

time: 40.4 us -> 37.3 us (0.923)
  Pallas kernels: 38.8 us -> 35.7 us
    pallas_call x1, Pallas kernels: 38.8 us -> 35.7 us  [on_device(): pl.pallas_call(functools.partial(ffn, R, T, UC), out_shape=jax.ShapeDtype...]
where the time goes in v2:
time: 37.3 us; the launch traced here: 37.1 us
  Pallas kernels  35.7 us (96%)
  local copies, waits for them, and re-layouts  1.39 us (4%)
    pallas_call x1, Pallas kernels, on_device(): pl.pallas_call(functools.partial(ffn, R, T, UC), out_shape=jax.ShapeDtype...  35.7 us
    unnamed x1, local copies, waits for them, and re-layouts  1.39 us

profile of v2, /device:TPU:0, one launch (start us, length us, event | category | flops | bytes accessed | tf_op | source)
XLA Modules:
  0.0 37.1 jit_solution(2058799744578518341)
XLA Ops:
  0.0 35.7 %shard_map.46 = bf16[4,4096]{1,0:T(4,128)(2,1)} custom-call(bf16[4,4096]{1,0:T(4,128)(2,1)} %tok.1, bf16[4096,1024]{1,0:T(8,128)(2,1)} %wg.1, bf16[4096,1024]{1,0:T(8,128)(2,1)} %wu.1, bf16[4096,1024]{1,0:T(8,128)(2,1)} %wd.1), custom_call_target="tpu_custom_call" | custom-call | tf_op jit(solution)/shard_map/pallas_call | solution.py:205
  35.7 1.4 %copy.6 = bf16[4,4096]{1,0:T(4,128)(2,1)} copy(bf16[4,4096]{1,0:T(4,128)(2,1)} %shard_map.46) | data formatting | bytes 65536
